TPU v7x, 128 devices: a whole 4x4x4 slice. The times are simulated.
128 devices in a mesh: dp: 8 (over z_hi, y), mp: 8 (over z_lo, x), outer: 2 (over core).
Axes of the slice: x: 4, y: 4, z: 4 (z_hi: 2, z_lo: 2; z = z_hi * 2 + z_lo), core: 2. Of those that a mesh axis runs over, the one named last changes fastest.
Arguments:
- activations: bfloat16 [32768, 8192], P(('dp', 'outer'), 'mp'), may hold values from -6 to 6
- act_scale: float32 [256, 64], P(('dp', 'outer'), 'mp'), may hold values from 0.25 to 4
- out_grads: bfloat16 [32768, 16384], P(('dp', 'outer'), 'mp'), may hold values from -6 to 6
- gradient_tile_scale: float32 [256, 128], P(('dp', 'outer'), 'mp'), may hold values from 0.25 to 4
- prior_input_factor: float32 [8, 1024, 1024], P('mp', ('dp', 'outer')), may hold values from -0.3 to 6, as said below
- g_factor: float32 [16, 1024, 1024], P('mp', ('dp', 'outer')), may hold values from -0.3 to 6, as said below
- weight_grad: bfloat16 [8192, 16384], P('mp', ('dp', 'outer')), may hold values from -6 to 6
- a_inverse: bfloat16 [8, 1024, 1024], P('mp', ('dp', 'outer')), as said below
- g_inverse: bfloat16 [16, 1024, 1024], P(('dp', 'outer'), 'mp'), as said below
Outputs:
- a_stat: float32 [8, 1024, 1024], P('mp', ('dp', 'outer'))
- g_stat: float32 [16, 1024, 1024], P('mp', ('dp', 'outer'))
- new_a_factor: float32 [8, 1024, 1024], P('mp', ('dp', 'outer'))
- new_g_factor: float32 [16, 1024, 1024], P('mp', ('dp', 'outer'))
- preconditioned: bfloat16 [8192, 16384], P('mp', ('dp', 'outer'))
Inputs may be any that keep to these rules, and one draw needn't show every extreme that they name: `a_inverse`: each block is the identity plus dense off-diagonal and diagonal entries of magnitude at most 1.5 / sqrt(1024). `g_inverse`: each block is the identity plus dense off-diagonal and diagonal entries of magnitude at most 1.5 / sqrt(1024). `prior_input_factor`: each block is symmetric with a positive diagonal. `g_factor`: each block is symmetric with a positive diagonal.
All inputs are finite; a program needn't handle non-finite values.
Results may differ from a plain program's by a relative error of at most 0.014.
Values may be sent and summed in bfloat16 or wider, within the bound.
A program may use at most 128 MiB of HBM per device.

v0:
```python
import jax
import jax.numpy as jnp
from jax import lax
from jax.sharding import PartitionSpec as P

BLK = 1024
QT = 128


EMA_DECAY = 0.95


def dequantize(quantized, tile_scale):
    row_total, column_total = quantized.shape
    tiles_with_scale = (
        quantized.reshape(row_total // QT, QT, column_total // QT, QT)
        * tile_scale[:, None, :, None]
    )
    return tiles_with_scale.reshape(row_total, column_total).astype(jnp.bfloat16)


def body(
    activations,
    act_scale,
    out_grads,
    gradient_tile_scale,
    prior_input_factor,
    g_factor,
    weight_grad,
    a_inverse,
    g_inverse,
):
    input_factor_tiles = dequantize(activations, act_scale).reshape(activations.shape[0], -1, BLK)
    gradient_factor_tiles = dequantize(out_grads, gradient_tile_scale).reshape(
        out_grads.shape[0], -1, BLK
    )
    input_count = input_factor_tiles.shape[1]
    activation_rows = jnp.einsum(
        "qym,qyx->myx", input_factor_tiles, input_factor_tiles, preferred_element_type=jnp.float32
    )
    gradient_rows = jnp.einsum(
        "qym,qyx->myx",
        gradient_factor_tiles,
        gradient_factor_tiles,
        preferred_element_type=jnp.float32,
    )
    summed = lax.psum_scatter(
        jnp.concatenate([activation_rows, gradient_rows], axis=1).astype(jnp.bfloat16),
        ("dp", "outer"),
        scatter_dimension=0,
        tiled=True,
    ).astype(jnp.float32)
    token_total = activations.shape[0] * lax.axis_size("dp") * lax.axis_size("outer")
    statistics = jnp.transpose(summed, (1, 0, 2)) / token_total
    a_stat = statistics[:input_count]
    g_stat = statistics[input_count:]
    new_a_factor = EMA_DECAY * prior_input_factor + (1.0 - EMA_DECAY) * a_stat
    new_g_factor = EMA_DECAY * g_factor + (1.0 - EMA_DECAY) * g_stat
    row_blocks = weight_grad.shape[0] // BLK
    column_blocks = weight_grad.shape[1] // BLK
    grad_blocks = weight_grad.reshape(row_blocks, BLK, column_blocks, BLK)
    right = jnp.einsum(
        "aigk,gkl->aigl",
        grad_blocks,
        lax.all_gather(g_inverse, "mp", axis=1, tiled=True),
        preferred_element_type=jnp.float32,
    ).astype(jnp.bfloat16)
    result = jnp.einsum(
        "aij,ajgl->aigl",
        lax.all_gather(a_inverse, ("dp", "outer"), axis=1, tiled=True),
        right,
        preferred_element_type=jnp.float32,
    ).astype(jnp.bfloat16)
    return (
        a_stat,
        g_stat,
        new_a_factor,
        new_g_factor,
        result.reshape(row_blocks * BLK, column_blocks * BLK),
    )


def solution(mesh):
    return jax.shard_map(
        body,
        mesh=mesh,
        in_specs=(
            P(("dp", "outer"), "mp"),
            P(("dp", "outer"), "mp"),
            P(("dp", "outer"), "mp"),
            P(("dp", "outer"), "mp"),
            P("mp", ("dp", "outer"), None),
            P("mp", ("dp", "outer"), None),
            P("mp", ("dp", "outer")),
            P("mp", ("dp", "outer"), None),
            P(("dp", "outer"), "mp", None),
        ),
        out_specs=(
            P("mp", ("dp", "outer"), None),
            P("mp", ("dp", "outer"), None),
            P("mp", ("dp", "outer"), None),
            P("mp", ("dp", "outer"), None),
            P("mp", ("dp", "outer")),
        ),
        check_vma=False,
    )
```

profile of v0, /device:TPU:1, one launch (start us, length us, event | category | flops | bytes accessed | tf_op | source)
XLA Modules:
  0.0 277.6 jit_solution(16005743546915442506)
XLA Ops:
  7.2 0.0 copy-start
  7.2 0.0 all-gather.3.cloned.1.call-start
  7.2 0.7 all-gather.3.cloned.1.call-update
  7.9 0.0 all-gather.5.cloned.1.call-start
  8.0 0.7 all-gather.5.cloned.1.call-update
  8.7 0.0 all-reduce.3.cloned.1.call-start
  8.7 0.8 copy.36
  9.5 0.6 mul.46
  10.1 0.0 copy-start.3
  10.1 9.6 %convert_bitcast_fusion.2 = bf16[1024,1,1024]{0,2,1:T(8,128)(2,1)S(1)} fusion(f32[256,8,8,128]{3,2,1,0:T(8,128)S(1)} %bitcast.55, bf16[2048,1024]{1,0:T(8,128)(2,1)} %param.9), kind=kOutput, calls=%fused_computation.17 | convolution fusion | flops 4302307328 | bytes 14680064 | tf_op jit(solution)/shard_map/qym,qyx->myx/dot_general | solution.py:38
  19.7 0.0 copy-done.3
  19.7 1.1 mul.49
  20.8 11.9 %fusion = bf16[2048,2048]{1,0:T(8,128)(2,1)} fusion(f32[256,8,16,128]{3,2,1,0:T(8,128)S(1)} %bitcast.54, bf16[2048,2048]{1,0:T(8,128)(2,1)} %param.11), kind=kLoop, calls=%fused_computation.1 | loop fusion | flops 12582912 | bytes 33554432 | tf_op jit(solution)/shard_map/convert_element_type | solution.py:19
  32.7 13.8 %convert_bitcast_fusion = bf16[1024,2,1024]{0,2,1:T(8,128)(2,1)S(1)} fusion(bf16[256,2,8,1024]{3,2,1,0:T(8,128)(2,1)} %bitcast.56), kind=kOutput, calls=%fused_computation.9 | convolution fusion | flops 8592031744 | bytes 12582912 | tf_op jit(solution)/shard_map/qym,qyx->myx/dot_general | solution.py:41
  46.5 3.2 %pad_maximum_fusion = bf16[1024,3,1024]{0,2,1:T(8,128)(2,1)} fusion(bf16[1024,2,1024]{0,2,1:T(8,128)(2,1)S(1)} %convert_bitcast_fusion, bf16[1024,1,1024]{0,2,1:T(8,128)(2,1)S(1)} %convert_bitcast_fusion.2), kind=kLoop, calls=%fused_computation.7 | loop fusion | flops 3145728 | bytes 12582912 | tf_op jit(solution)/shard_map/concatenate | solution.py:48
  49.7 14.4 %copy.39 = bf16[1024,3,1024]{2,1,0:T(4,128)(2,1)} copy(bf16[1024,3,1024]{0,2,1:T(8,128)(2,1)} %pad_maximum_fusion) | data formatting | bytes 12582912 | tf_op jit(solution)/shard_map/concatenate | solution.py:48
  64.1 0.0 copy-start.4
  64.1 0.0 all-reduce.3.cloned.1.call-update
  64.1 0.6 copy-done.4
  64.8 0.6 dynamic-slice
  66.0 0.0 all-gather.3.cloned.1.call-done
  66.0 38.5 %all-gather.5.cloned.1.call-done = bf16[1,1024,1024]{2,1,0:T(8,128)(2,1)} async-done(((bf16[1,64,1024]{2,1,0:T(8,128)(2,1)}), bf16[1,1024,1024]{2,1,0:T(8,128)(2,1)}) %all-gather.5.cloned.1.call-update) | async-done | bytes 2097168 | tf_op jit(solution)/shard_map/all_gather | solution.py:70
  104.6 0.0 copy-done
  104.6 8.1 %convert_bitcast_fusion.1 = bf16[1024,1024]{0,1:T(8,128)(2,1)} fusion(bf16[1,1024,1024]{2,1,0:T(8,128)(2,1)} %all-gather.5.cloned.1.call-done, bf16[1024,1024]{1,0:T(8,128)(2,1)S(1)} %copy-done, bf16[1,1024,1024]{2,1,0:T(8,128)(2,1)} %all-gather.3.cloned.1.call-done), kind=kOutput, calls=%fused_computation.15 | convolution fusion | flops 4297064448 | bytes 8388608 | tf_op jit(solution)/shard_map/aij,ajgl->aigl/dot_general | solution.py:68
  112.7 0.0 copy-start.1
  112.7 0.0 copy-start.2
  112.7 4.0 %copy.41 = bf16[1024,1024]{1,0:T(8,128)(2,1)} copy(bf16[1024,1024]{0,1:T(8,128)(2,1)} %convert_bitcast_fusion.1) | data formatting | bytes 4194304
  116.7 151.0 %all-reduce.3.cloned.1.call-done = bf16[1024,3,1024]{2,1,0:T(4,128)(2,1)} async-done(((bf16[1024,3,1024]{2,1,0:T(4,128)(2,1)}), bf16[1024,3,1024]{2,1,0:T(4,128)(2,1)}) %all-reduce.3.cloned.1.call-update) | async-done | bytes 6291472
  267.8 1.2 constant_dynamic-slice_fusion
  269.0 0.2 multiply_bitcast_fusion
  269.2 0.0 copy-done.1
  269.2 1.1 multiply_add_fusion
  270.3 0.0 copy-done.2
  270.3 0.8 multiply_add_fusion.1
Async XLA Ops:
  7.2 97.4 %copy-start = (bf16[1024,1024]{1,0:T(8,128)(2,1)S(1)}, bf16[1024,1024]{1,0:T(8,128)(2,1)}, u32[]{:S(2)}) copy-start(bf16[1024,1024]{1,0:T(8,128)(2,1)} %param.15) | copy-start | bytes 6291460
  7.2 58.8 %all-gather.3.cloned.1.call-start = ((), (), s32[]{:S(2)}) async-start(), calls=%async_computation | async-start | bytes 2359296 | tf_op jit(solution)/shard_map/all_gather | solution.py:65
  7.9 96.6 %all-gather.5.cloned.1.call-start = ((), (), s32[]{:S(2)}) async-start(), calls=%async_computation.1 | async-start | bytes 2228224 | tf_op jit(solution)/shard_map/all_gather | solution.py:70
  8.7 259.1 %all-reduce.3.cloned.1.call-start = ((), (), s32[]{:S(2)}) async-start(), calls=%async_computation.2 | async-start | bytes 16777216
  10.1 9.6 %copy-start.3 = (f32[16,16]{1,0:T(8,128)S(1)}, f32[16,16]{1,0:T(8,128)}, u32[]{:S(2)}) copy-start(f32[16,16]{1,0:T(8,128)} %param.12) | copy-start | bytes 3076
  64.1 0.7 copy-start.4
  112.7 156.5 %copy-start.1 = (f32[2,64,1024]{2,1,0:T(8,128)S(1)}, f32[2,64,1024]{2,1,0:T(8,128)}, u32[]{:S(2)}) copy-start(f32[2,64,1024]{2,1,0:T(8,128)} %param.14) | copy-start | bytes 1572868
  112.7 157.6 %copy-start.2 = (f32[1,64,1024]{2,1,0:T(8,128)S(1)}, f32[1,64,1024]{2,1,0:T(8,128)}, u32[]{:S(2)}) copy-start(f32[1,64,1024]{2,1,0:T(8,128)} %param.13) | copy-start | bytes 786436
Sparse Core Ops, SparseCore 0:
  9.6 39.1 all-gather.2
  51.2 53.2 all-gather.4
  107.1 160.6 all-reduce.2
where the time goes:
time: 279 us; the launch traced here: 278 us
  waiting for transfers between devices  191 us (68%)
  matrix products  31.5 us (11%)
  local copies, waits for them, and re-layouts  23.4 us (8%)
  other arithmetic  17.2 us (6%)
  between operations  14.5 us (5%)
    unnamed x4, waiting for transfers between devices  152 us
    all_gather x1, waiting for transfers between devices, body(): lax.all_gather(a_inverse, ('dp', 'outer'), axis=1, tiled=True)  38.5 us
    concatenate x1, local copies, waits for them, and re-layouts, body(): jnp.concatenate([activation_rows, gradient_rows], axis=1)  14.4 us
    dot_general x1, matrix products, body(): jnp.einsum('qym,qyx->myx', gradient_factor_tiles, gradient_factor_tiles,...  13.8 us
    convert_element_type x1, other arithmetic, dequantize(): tiles_with_scale.reshape(row_total, column_total).astype(jnp.bfloat16)  11.9 us
    dot_general x1, matrix products, body(): jnp.einsum('qym,qyx->myx', input_factor_tiles, input_factor_tiles, prefer...  9.55 us
    dot_general x1, matrix products, body(): jnp.einsum('aij,ajgl->aigl', lax.all_gather(a_inverse, ('dp', 'outer'), a...  8.1 us
    unnamed x14, local copies, waits for them, and re-layouts  7.26 us
  transfers between devices with their start and end apart: 3, of which 2 were waited for; matrix products, arithmetic and copies ran while one was open for 25% of the time, Pallas kernels for 0%

commit v1 on v0

v1 whole, which is shorter than its diff:
```python
import jax
import jax.numpy as jnp
from jax import lax
from jax.experimental import pallas as pl
from jax.experimental.pallas import tpu as pltpu
from jax.sharding import PartitionSpec as P

BLK = 1024
QT = 128
EMA_DECAY = 0.95

MESH = pl.DeviceIdType.MESH
NB = 3
STRIPS = 8
KEPT = 5
WIDE = KEPT * QT
CHUNK = 256


def kernel(
    act_scale,
    grad_scale,
    act_hbm,
    grads_hbm,
    weight_hbm,
    a_inv_hbm,
    g_inv_hbm,
    a_out,
    g_out,
    pre_out,
    raw,
    deq,
    deq_t,
    parts,
    swapped,
    chip_sums,
    arrived,
    sums,
    mirror_out,
    mirror_in,
    turned,
    g_full,
    a_full,
    weight,
    right,
    load_sem,
    own_sem,
    g_send,
    g_recv,
    a_send,
    a_recv,
    swap_send,
    swap_recv,
    rs_send,
    rs_recv,
    mir_send,
    mir_recv,
):
    dp = lax.axis_index("dp")
    mp = lax.axis_index("mp")
    core = lax.axis_index("outer")
    y = lax.rem(dp, 4)
    x = lax.rem(mp, 4)
    tokens = act_hbm.shape[0]
    chunks = tokens // CHUNK
    tiles = tokens // QT

    def strip_of(offset):
        return lax.rem(dp + offset, STRIPS)

    def y_peer(offset):
        return dp - y + lax.rem(y + offset, 4)

    def x_peer(offset):
        return mp - x + lax.rem(x + offset, 4)

    def z_far(index):
        return lax.rem(index + 4, 8)

    def load(b, k):
        rows = pl.ds(pl.multiple_of(k * CHUNK, CHUNK), CHUNK)
        if b == 0:
            source = act_hbm.at[rows, :]
        else:
            source = grads_hbm.at[rows, pl.ds((b - 1) * BLK, BLK)]
        return pltpu.make_async_copy(source, raw.at[b, rows, :], load_sem.at[b, k])

    def g_rows(slot):
        return g_full.at[pl.ds(pl.multiple_of(slot * 128, 128), 128), :]

    def a_rows(strip, half):
        return a_full.at[pl.ds(pl.multiple_of(strip * 128 + half * 64, 64), 64), :]

    own_g = pltpu.make_async_copy(g_inv_hbm.at[0], g_rows(mp), own_sem.at[0])
    own_a = pltpu.make_async_copy(a_inv_hbm.at[0], a_rows(dp, core), own_sem.at[1])
    own_w = pltpu.make_async_copy(weight_hbm, weight, own_sem.at[2])
    own_g.start()
    own_a.start()
    for k in range(chunks):
        load(0, k).start()

    barrier = pltpu.get_barrier_semaphore()
    for offset in range(STRIPS):
        for other in range(2):
            if (offset, other) != (0, 0):
                pl.semaphore_signal(
                    barrier,
                    inc=1,
                    device_id={"dp": strip_of(offset), "outer": lax.rem(core + other, 2)},
                    device_id_type=MESH,
                )
    for offset in (1, 2, 3):
        pl.semaphore_signal(barrier, inc=1, device_id={"mp": x_peer(offset)}, device_id_type=MESH)
    pl.semaphore_signal(barrier, inc=1, device_id={"mp": z_far(mp)}, device_id_type=MESH)
    for b in (1, 2):
        for k in range(chunks):
            load(b, k).start()
    own_w.start()
    own_g.wait()
    own_a.wait()
    pl.semaphore_wait(barrier, 2 * STRIPS - 1 + 4)

    def g_copy(slot, kind, peer):
        rows = g_rows(slot)
        return pltpu.make_async_remote_copy(
            rows, rows, g_send.at[kind], g_recv.at[kind],
            device_id={"mp": peer}, device_id_type=MESH,
        )

    def a_copy(strip, half, kind, peer):
        rows = a_rows(strip, half)
        return pltpu.make_async_remote_copy(
            rows, rows, a_send.at[kind], a_recv.at[kind],
            device_id=peer, device_id_type=MESH,
        )

    g_far = g_copy(mp, 0, z_far(mp))
    a_far = a_copy(dp, core, 0, {"dp": z_far(dp)})
    g_near = [g_copy(mp, o, x_peer(o)) for o in (1, 2, 3)]
    a_near = [a_copy(dp, core, o, {"dp": y_peer(o)}) for o in (1, 2, 3)]
    a_pair = [a_copy(dp, core, 7, {"outer": 1 - core})]
    g_far.start()
    a_far.start()
    for o in (0, 2, 1):
        g_near[o].start()
        a_near[o].start()
    a_pair[0].start()
    g_next = [g_copy(z_far(mp), 3 + o, x_peer(o)) for o in (1, 2, 3)]
    a_next = [a_copy(z_far(dp), core, 3 + o, {"dp": y_peer(o)}) for o in (1, 2, 3)]

    def dequantize(b):
        def one(k, carry):
            rows = pl.ds(pl.multiple_of(k * QT, QT), QT)
            for t in range(BLK // QT):
                scale = jnp.where(
                    b == 0, act_scale[k, t], grad_scale[k, jnp.maximum(b - 1, 0) * 8 + t]
                )
                cols = slice(t * QT, (t + 1) * QT)
                value = (raw[b, rows, cols].astype(jnp.float32) * scale).astype(jnp.bfloat16)
                deq[rows, cols] = value
                flipped = value.T
                deq_t[(t + 4) * QT : (t + 5) * QT, rows] = flipped
                if t >= 4:
                    deq_t[(t - 4) * QT : (t - 3) * QT, rows] = flipped
            return carry

        def group(g, carry):
            for bb in range(NB):
                @pl.when(b == bb)
                def _():
                    load(bb, g).wait()

            return lax.fori_loop(g * (CHUNK // QT), (g + 1) * (CHUNK // QT), one, carry)

        lax.fori_loop(0, chunks, group, 0)

    def gram(b):
        def one(j, carry):
            lhs = deq_t[pl.ds(pl.multiple_of(j * 256, 256), 768), :]
            rhs = deq[:, pl.ds(pl.multiple_of(j * 256, 256), 256)]
            tile = jnp.dot(lhs, rhs, preferred_element_type=jnp.float32).astype(jnp.bfloat16)
            for i in range(6):
                strip = lax.rem(2 * j + 4 + i, STRIPS)
                for t in range(2):
                    d = 4 - i + t
                    if 0 <= d < KEPT:
                        for half in range(2):
                            top = i * QT + half * 64
                            parts[half, b, strip, :, d * QT : (d + 1) * QT] = tile[
                                top : top + 64, t * QT : (t + 1) * QT
                            ]
            return carry

        lax.fori_loop(0, 4, one, 0)

    def swap(b):
        return pltpu.make_async_remote_copy(
            parts.at[1 - core, b], swapped.at[b], swap_send.at[b], swap_recv.at[b],
            device_id={"outer": 1 - core}, device_id_type=MESH,
        )

    def scatter(b, offset):
        return pltpu.make_async_remote_copy(
            chip_sums.at[b, strip_of(offset)], arrived.at[offset - 1, b],
            rs_send.at[b, offset - 1], rs_recv.at[b, offset - 1],
            device_id={"dp": strip_of(offset)}, device_id_type=MESH,
        )

    def chip_sum(b):
        swap(b).wait()

        def one(q, carry):
            total = parts[core, b, q].astype(jnp.float32) + swapped[b, q].astype(jnp.float32)
            chip_sums[b, q] = total.astype(jnp.bfloat16)
            return carry

        lax.fori_loop(0, STRIPS, one, 0)
        for offset in (4, 1, 3, 5, 7, 2, 6):
            scatter(b, offset).start()

    def block(b, carry):
        dequantize(b)

        @pl.when(b > 0)
        def _():
            chip_sum(b - 1)

        gram(b)
        swap(b).start()

        @pl.when(b == 0)
        def _():
            g_far.wait()
            a_far.wait()
            for o in (0, 2, 1):
                g_next[o].start()
                a_next[o].start()

        return carry

    lax.fori_loop(0, NB, block, 0)
    chip_sum(NB - 1)

    a_pair.append(a_copy(z_far(dp), core, 8, {"outer": 1 - core}))
    a_pair[-1].start()
    for o in (1, 2, 3):
        a_near[o - 1].wait()
        a_pair.append(a_copy(y_peer(4 - o), core, 8 + o, {"outer": 1 - core}))
        a_pair[-1].start()
    for o in (1, 2, 3):
        a_next[o - 1].wait()
        a_pair.append(a_copy(z_far(y_peer(4 - o)), core, 11 + o, {"outer": 1 - core}))
        a_pair[-1].start()
    for o in (1, 2, 3):
        g_near[o - 1].wait()
        g_next[o - 1].wait()
    for copy in a_pair:
        copy.wait()
    own_w.wait()

    def precondition(n, carry):
        cols = pl.ds(pl.multiple_of(n * 256, 256), 256)
        right[...] = jnp.dot(
            weight[...], g_full[:, cols], preferred_element_type=jnp.float32
        ).astype(jnp.bfloat16)
        pre_out[:, cols] = jnp.dot(
            a_full[...], right[...], preferred_element_type=jnp.float32
        ).astype(jnp.bfloat16)
        return carry

    lax.fori_loop(0, 4, precondition, 0)

    def mirror(b, d, other):
        to_core = lax.rem(core + other, 2)
        return pltpu.make_async_remote_copy(
            mirror_out.at[b, d - 1],
            mirror_in.at[b, d - 1, pl.ds(pl.multiple_of(core * 64, 64), 64), :],
            mir_send.at[b, d - 1, other], mir_recv.at[b, d - 1, other],
            device_id={"dp": strip_of(d), "outer": to_core}, device_id_type=MESH,
        )

    def finish(b, carry):
        for offset in range(1, STRIPS):
            scatter(b, offset).wait()
        total = chip_sums[b, dp].astype(jnp.float32)
        for offset in range(1, STRIPS):
            total = total + arrived[offset - 1, b].astype(jnp.float32)
        for d in range(KEPT):
            cols = pl.ds(pl.multiple_of(strip_of(d) * QT, QT), QT)
            piece = total[:, d * QT : (d + 1) * QT]
            sums[b, :, cols] = piece
            if 1 <= d <= 3:
                mirror_out[b, d - 1] = piece.astype(jnp.bfloat16)
        for d in (1, 2, 3):
            for other in range(2):
                mirror(b, d, other).start()
        return carry

    lax.fori_loop(0, NB, finish, 0)

    def last(b, carry):
        for d in (1, 2, 3):
            for other in range(2):
                mirror(b, d, other).wait()
        for d in (1, 2, 3):
            turned[...] = mirror_in[b, d - 1].astype(jnp.float32).T
            cols = pl.ds(pl.multiple_of(strip_of(STRIPS - d) * QT, QT), QT)
            sums[b, :, cols] = turned[pl.ds(pl.multiple_of(core * 64, 64), 64), :]
        return carry

    lax.fori_loop(0, NB, last, 0)
    a_out[0] = sums[0]
    g_out[0] = sums[1]
    g_out[1] = sums[2]


def body(
    activations,
    act_scale,
    out_grads,
    gradient_tile_scale,
    prior_input_factor,
    g_factor,
    weight_grad,
    a_inverse,
    g_inverse,
):
    tokens = activations.shape[0]
    token_total = tokens * lax.axis_size("dp") * lax.axis_size("outer")
    vmem = pl.BlockSpec(memory_space=pltpu.VMEM)
    smem = pl.BlockSpec(memory_space=pltpu.SMEM)
    anywhere = pl.BlockSpec(memory_space=pl.ANY)
    bf16, f32 = jnp.bfloat16, jnp.float32
    dma = pltpu.SemaphoreType.DMA
    a_sum, g_sum, preconditioned = pl.pallas_call(
        kernel,
        out_shape=(
            jax.ShapeDtypeStruct((1, 64, BLK), f32),
            jax.ShapeDtypeStruct((2, 64, BLK), f32),
            jax.ShapeDtypeStruct((BLK, BLK), bf16),
        ),
        in_specs=[smem, smem] + [anywhere] * 5,
        out_specs=(vmem, vmem, vmem),
        scratch_shapes=[
            pltpu.VMEM((NB, tokens, BLK), bf16),
            pltpu.VMEM((tokens, BLK), bf16),
            pltpu.VMEM((12 * QT, tokens), bf16),
            pltpu.VMEM((2, NB, STRIPS, 64, WIDE), bf16),
            pltpu.VMEM((NB, STRIPS, 64, WIDE), bf16),
            pltpu.VMEM((NB, STRIPS, 64, WIDE), bf16),
            pltpu.VMEM((STRIPS - 1, NB, 64, WIDE), bf16),
            pltpu.VMEM((NB, 64, BLK), f32),
            pltpu.VMEM((NB, 3, 64, QT), bf16),
            pltpu.VMEM((NB, 3, QT, QT), bf16),
            pltpu.VMEM((QT, QT), f32),
            pltpu.VMEM((BLK, BLK), bf16),
            pltpu.VMEM((BLK, BLK), bf16),
            pltpu.VMEM((BLK, BLK), bf16),
            pltpu.VMEM((BLK, 256), bf16),
            dma((NB, tokens // CHUNK)),
            dma((3,)),
            dma((7,)),
            dma((7,)),
            dma((15,)),
            dma((15,)),
            dma((NB,)),
            dma((NB,)),
            dma((NB, STRIPS - 1)),
            dma((NB, STRIPS - 1)),
            dma((NB, 3, 2)),
            dma((NB, 3, 2)),
        ],
        compiler_params=pltpu.CompilerParams(
            collective_id=0, has_side_effects=True, vmem_limit_bytes=56 << 20
        ),
        cost_estimate=pl.CostEstimate(
            flops=14_000_000_000, bytes_accessed=20_000_000, transcendentals=0
        ),
    )(
        act_scale,
        gradient_tile_scale,
        activations,
        out_grads,
        weight_grad,
        a_inverse,
        g_inverse,
    )
    a_stat = a_sum / token_total
    g_stat = g_sum / token_total
    new_a_factor = EMA_DECAY * prior_input_factor + (1.0 - EMA_DECAY) * a_stat
    new_g_factor = EMA_DECAY * g_factor + (1.0 - EMA_DECAY) * g_stat
    return a_stat, g_stat, new_a_factor, new_g_factor, preconditioned


def solution(mesh):
    return jax.shard_map(
        body,
        mesh=mesh,
        in_specs=(
            P(("dp", "outer"), "mp"),
            P(("dp", "outer"), "mp"),
            P(("dp", "outer"), "mp"),
            P(("dp", "outer"), "mp"),
            P("mp", ("dp", "outer"), None),
            P("mp", ("dp", "outer"), None),
            P("mp", ("dp", "outer")),
            P("mp", ("dp", "outer"), None),
            P(("dp", "outer"), "mp", None),
        ),
        out_specs=(
            P("mp", ("dp", "outer"), None),
            P("mp", ("dp", "outer"), None),
            P("mp", ("dp", "outer"), None),
            P("mp", ("dp", "outer"), None),
            P("mp", ("dp", "outer")),
        ),
        check_vma=False,
    )
```

time: 279 us -> 67.6 us (0.24)
  waiting for transfers between devices: 191 us -> 0 us
  Pallas kernels: 0 us -> 59.9 us
  matrix products: 31.5 us -> 0 us
  local copies, waits for them, and re-layouts: 23.4 us -> 2.69 us
  between operations: 14.5 us -> 0.66 us
  other arithmetic: 17.2 us -> 4.14 us
    unnamed x4 -> x0, waiting for transfers between devices: 152 us -> none
    pallas_call x0 -> x1, Pallas kernels: none -> 59.9 us  [body(): pl.pallas_call(kernel, out_shape=(jax.ShapeDtypeStruct((1, 64, BLK), f32)...]
    all_gather x2 -> x0, waiting for transfers between devices: 38.6 us -> none  [the longest x1 38.5 us: body(): lax.all_gather(a_inverse, ('dp', 'outer'), axis=1, tiled=True)]
    dot_general x3 -> x0, matrix products: 31.5 us -> none  [the longest x1 13.8 us: body(): jnp.einsum('qym,qyx->myx', gradient_factor_tiles, gradient_factor_tiles,...]
    concatenate x1 -> x0, local copies, waits for them, and re-layouts: 14.4 us -> none  [body(): jnp.concatenate([activation_rows, gradient_rows], axis=1)]
    convert_element_type x1 -> x0, other arithmetic: 11.9 us -> none  [dequantize(): tiles_with_scale.reshape(row_total, column_total).astype(jnp.bfloat16)]
    unnamed x14 -> x8, local copies, waits for them, and re-layouts: 7.26 us -> 2.69 us
    concatenate x1 -> x0, other arithmetic: 3.22 us -> none  [body(): jnp.concatenate([activation_rows, gradient_rows], axis=1)]
  transfers between devices with their start and end apart: 3 -> 0, of which waited for: 2 -> 0; matrix products, arithmetic and copies ran while one was open for 25% -> 0% of each run, Pallas kernels for 0% -> 0%
where the time goes in v1:
time: 67.6 us; the launch traced here: 67.4 us
  Pallas kernels  59.9 us (89%)
  other arithmetic  4.14 us (6%)
  local copies, waits for them, and re-layouts  2.69 us (4%)
    pallas_call x1, Pallas kernels, body(): pl.pallas_call(kernel, out_shape=(jax.ShapeDtypeStruct((1, 64, BLK), f32)...  59.9 us
    unnamed x8, local copies, waits for them, and re-layouts  2.69 us
    add x1, other arithmetic, body(): new_g_factor = EMA_DECAY * g_factor + (1.0 - EMA_DECAY) * g_stat  2.19 us
    add x1, other arithmetic, body(): new_a_factor = EMA_DECAY * prior_input_factor + (1.0 - EMA_DECAY) * a_stat  1.95 us

profile of v1, /device:TPU:1, one launch (start us, length us, event | category | flops | bytes accessed | tf_op | source)
XLA Modules:
  0.0 67.4 jit_solution(14234855823658765546)
XLA Ops:
  0.6 1.4 %copy.14.act_scale = f32[16,8]{1,0:T(8,128)} copy(f32[16,8]{0,1:T(8,128)} %param.10) | data formatting | bytes 1024 | tf_op args[1]
  2.0 0.0 copy-start.2
  2.0 0.0 copy-start.1
  2.0 59.9 %shard_map.128 = (f32[1,64,1024]{2,1,0:T(8,128)}, f32[2,64,1024]{2,1,0:T(8,128)}, bf16[1024,1024]{1,0:T(8,128)(2,1)}) custom-call(f32[16,8]{1,0:T(8,128)} %copy.14.act_scale, f32[16,16]{1,0:T(8,128)} %grad_scale.1, bf16[2048,1024]{1,0:T(8,128)(2,1)} %act_hbm.1, bf16[2048,2048]{1,0:T(8,128)(2,1)} %grads_hbm.1, bf16[1024,1024]{1,0:T(8,128)(2,1)} %weight_hbm.1, ...), custom_call_target="tpu_custom_call" | custom-call | flops 14000000000 | bytes 20000000 | tf_op jit(solution)/shard_map/pallas_call | solution.py:335
  61.9 0.0 copy-start
  61.9 0.0 copy-done.2
  61.9 1.9 %multiply_add_fusion.1 = (f32[1,64,1024]{2,1,0:T(8,128)}, f32[1,64,1024]{2,1,0:T(8,128)}) fusion(f32[1,64,1024]{2,1,0:T(8,128)} %get-tuple-element.8, f32[1,64,1024]{2,1,0:T(8,128)S(1)} %copy-done.2), kind=kLoop, calls=%fused_computation.1 | loop fusion | flops 262144 | bytes 1048576 | tf_op jit(solution)/shard_map/add | solution.py:390
  63.9 0.0 copy-done.1
  63.9 2.2 %multiply_add_fusion = (f32[2,64,1024]{2,1,0:T(8,128)}, f32[2,64,1024]{2,1,0:T(8,128)}) fusion(f32[2,64,1024]{2,1,0:T(8,128)} %get-tuple-element.9, f32[2,64,1024]{2,1,0:T(8,128)S(1)} %copy-done.1), kind=kLoop, calls=%fused_computation | loop fusion | flops 524288 | bytes 2097152 | tf_op jit(solution)/shard_map/add | solution.py:391
  66.1 0.0 copy-done
  66.1 1.3 %copy.16 = bf16[1024,1024]{1,0:T(8,128)(2,1)} copy(bf16[1024,1024]{1,0:T(8,128)(2,1)S(1)} %copy-done) | data formatting | bytes 4194304
Async XLA Ops:
  2.0 59.9 %copy-start.2 = (f32[1,64,1024]{2,1,0:T(8,128)S(1)}, f32[1,64,1024]{2,1,0:T(8,128)}, u32[]{:S(2)}) copy-start(f32[1,64,1024]{2,1,0:T(8,128)} %param.13) | copy-start | bytes 786436
  2.0 61.9 %copy-start.1 = (f32[2,64,1024]{2,1,0:T(8,128)S(1)}, f32[2,64,1024]{2,1,0:T(8,128)}, u32[]{:S(2)}) copy-start(f32[2,64,1024]{2,1,0:T(8,128)} %param.14) | copy-start | bytes 1572868
  61.9 4.2 %copy-start = (bf16[1024,1024]{1,0:T(8,128)(2,1)S(1)}, bf16[1024,1024]{1,0:T(8,128)(2,1)}, u32[]{:S(2)}) copy-start(bf16[1024,1024]{1,0:T(8,128)(2,1)} %get-tuple-element.24) | copy-start | bytes 6291460

commit v2 on v1

v2 whole, which is shorter than its diff:
```python
import functools

import jax
import jax.numpy as jnp
from jax import lax
from jax.experimental import pallas as pl
from jax.experimental.pallas import tpu as pltpu
from jax.sharding import PartitionSpec as P

BLK = 1024
QT = 128
EMA_DECAY = 0.95

MESH = pl.DeviceIdType.MESH
NB = 3
STRIPS = 8
KEPT = 5
WIDE = KEPT * QT
AROUND = (1, 3, 2)
CHUNK = 512


def kernel(
    act_scale_hbm,
    grad_scale_hbm,
    act_hbm,
    grads_hbm,
    weight_hbm,
    a_inv_hbm,
    g_inv_hbm,
    a_out,
    g_out,
    pre_out,
    act_scale,
    grad_scale,
    raw,
    deq_even,
    deq_odd,
    flip_even,
    flip_odd,
    parts,
    swapped,
    chip_sums,
    first_in,
    middle,
    second_in,
    own_sum,
    sums,
    mirror_out,
    mirror_in,
    turned,
    g_full,
    a_full,
    weight,
    right,
    load_sem,
    own_sem,
    g_send,
    g_recv,
    a_send,
    a_recv,
    swap_send,
    swap_recv,
    first_send,
    first_recv,
    second_send,
    second_recv,
    mir_send,
    mir_recv,
):
    dp = lax.axis_index("dp")
    mp = lax.axis_index("mp")
    core = lax.axis_index("outer")
    y = lax.rem(dp, 4)
    x = lax.rem(mp, 4)
    z_half = dp // 4
    tokens = act_hbm.shape[0]
    chunks = tokens // CHUNK
    tiles = tokens // QT

    def strip_of(offset):
        return lax.rem(dp + offset, STRIPS)

    def y_peer(offset):
        return dp - y + lax.rem(y + offset, 4)

    def x_peer(offset):
        return mp - x + lax.rem(x + offset, 4)

    def z_far(index):
        return lax.rem(index + 4, 8)

    def load(b, k):
        rows = pl.ds(pl.multiple_of(k * CHUNK, CHUNK), CHUNK)
        if b == 0:
            source = act_hbm.at[rows, :]
        else:
            source = grads_hbm.at[rows, pl.ds((b - 1) * BLK, BLK)]
        return pltpu.make_async_copy(source, raw.at[b % 2, rows, :], load_sem.at[b, k])

    def g_rows(slot):
        return g_full.at[pl.ds(pl.multiple_of(slot * 128, 128), 128), :]

    def a_rows(strip, half):
        return a_full.at[pl.ds(pl.multiple_of(strip * 128 + half * 64, 64), 64), :]

    own_g = pltpu.make_async_copy(g_inv_hbm.at[0], g_rows(mp), own_sem.at[0])
    own_a = pltpu.make_async_copy(a_inv_hbm.at[0], a_rows(dp, core), own_sem.at[1])
    own_w = pltpu.make_async_copy(weight_hbm, weight, own_sem.at[2])
    own_scales = (
        pltpu.make_async_copy(act_scale_hbm, act_scale, own_sem.at[3]),
        pltpu.make_async_copy(grad_scale_hbm, grad_scale, own_sem.at[4]),
    )
    for copy in own_scales:
        copy.start()
    own_g.start()
    own_a.start()
    for k in range(chunks):
        load(0, k).start()

    barrier = pltpu.get_barrier_semaphore()
    for offset in range(STRIPS):
        for other in range(2):
            if (offset, other) != (0, 0):
                pl.semaphore_signal(
                    barrier,
                    inc=1,
                    device_id={"dp": strip_of(offset), "outer": lax.rem(core + other, 2)},
                    device_id_type=MESH,
                )
    for offset in (1, 2, 3):
        pl.semaphore_signal(barrier, inc=1, device_id={"mp": x_peer(offset)}, device_id_type=MESH)
    pl.semaphore_signal(barrier, inc=1, device_id={"mp": z_far(mp)}, device_id_type=MESH)
    for k in range(chunks):
        load(1, k).start()
    own_w.start()
    own_g.wait()
    own_a.wait()
    for copy in own_scales:
        copy.wait()
    pl.semaphore_wait(barrier, 2 * STRIPS - 1 + 4)

    def g_copy(slot, kind, peer):
        rows = g_rows(slot)
        return pltpu.make_async_remote_copy(
            rows, rows, g_send.at[kind], g_recv.at[kind],
            device_id={"mp": peer}, device_id_type=MESH,
        )

    def a_copy(strip, half, kind, peer):
        rows = a_rows(strip, half)
        return pltpu.make_async_remote_copy(
            rows, rows, a_send.at[kind], a_recv.at[kind],
            device_id=peer, device_id_type=MESH,
        )

    g_far = g_copy(mp, 0, z_far(mp))
    a_far = a_copy(dp, core, 0, {"dp": z_far(dp)})
    g_near = [g_copy(mp, o, x_peer(o)) for o in (1, 2, 3)]
    a_near = [a_copy(dp, core, o, {"dp": y_peer(o)}) for o in (1, 2, 3)]
    a_pair = [a_copy(dp, core, 7, {"outer": 1 - core})]
    a_far.start()
    g_far.start()
    for o in (0, 2, 1):
        g_near[o].start()
        a_near[o].start()
    a_pair[0].start()
    g_next = [g_copy(z_far(mp), 3 + o, x_peer(o)) for o in (1, 2, 3)]
    a_next = [a_copy(z_far(dp), core, 3 + o, {"dp": y_peer(o)}) for o in (1, 2, 3)]

    deqs = (deq_even, deq_odd)
    flips = (flip_even, flip_odd)

    def dequantize(b, k):
        for inner in range(CHUNK // QT):
            tile_row = k * (CHUNK // QT) + inner
            rows = pl.ds(pl.multiple_of(tile_row * QT, QT), QT)
            for t in range(BLK // QT):
                scale = act_scale[t, tile_row] if b == 0 else grad_scale[tile_row, (b - 1) * 8 + t]
                cols = slice(t * QT, (t + 1) * QT)
                value = (raw[b % 2, rows, cols].astype(jnp.float32) * scale).astype(jnp.bfloat16)
                deqs[b % 2][rows, cols] = value
                flipped = value.T
                flips[b % 2][(t + 4) * QT : (t + 5) * QT, rows] = flipped
                if t >= 4:
                    flips[b % 2][(t - 4) * QT : (t - 3) * QT, rows] = flipped

    def gram(b, j):
        lhs = flips[b % 2][pl.ds(pl.multiple_of(j * 256, 256), 768), :]
        rhs = deqs[b % 2][:, pl.ds(pl.multiple_of(j * 256, 256), 256)]
        tile = jnp.dot(lhs, rhs, preferred_element_type=jnp.float32).astype(jnp.bfloat16)
        for i in range(6):
            strip = lax.rem(2 * j + 4 + i, STRIPS)
            for t in range(2):
                d = 4 - i + t
                if 0 <= d < KEPT:
                    for half in range(2):
                        top = i * QT + half * 64
                        parts[half, b, strip, :, d * QT : (d + 1) * QT] = tile[
                            top : top + 64, t * QT : (t + 1) * QT
                        ]

    def swap(b):
        return pltpu.make_async_remote_copy(
            parts.at[1 - core, b], swapped.at[b], swap_send.at[b], swap_recv.at[b],
            device_id={"outer": 1 - core}, device_id_type=MESH,
        )

    def first_ring(b, o):
        return pltpu.make_async_remote_copy(
            chip_sums.at[b, :, lax.rem(y + o, 4)], first_in.at[b, pl.ds(2 * (o - 1), 2)],
            first_send.at[b, o - 1], first_recv.at[b, o - 1],
            device_id={"dp": y_peer(o)}, device_id_type=MESH,
        )

    def first_far(b):
        return pltpu.make_async_remote_copy(
            chip_sums.at[b, 1 - z_half], first_in.at[b, pl.ds(0, 4)],
            first_send.at[b, 3], first_recv.at[b, 3],
            device_id={"dp": z_far(dp)}, device_id_type=MESH,
        )

    def second_ring(b, o):
        return pltpu.make_async_remote_copy(
            middle.at[b, o], second_in.at[b, o - 1],
            second_send.at[b, o - 1], second_recv.at[b, o - 1],
            device_id={"dp": y_peer(o)}, device_id_type=MESH,
        )

    def second_far(b):
        return pltpu.make_async_remote_copy(
            middle.at[b, 1], second_in.at[b, 0], second_send.at[b, 3], second_recv.at[b, 3],
            device_id={"dp": z_far(dp)}, device_id_type=MESH,
        )

    def wide(value):
        return value.astype(jnp.float32)

    def chip_sum(b):
        swap(b).wait()

        def one(q, carry):
            total = wide(parts[core, b, q]) + wide(swapped[b, q])
            chip_sums[b, q // 4, lax.rem(q, 4)] = total.astype(jnp.bfloat16)
            return carry

        lax.fori_loop(0, STRIPS, one, 0)

        @pl.when(core == 0)
        def _():
            for o in AROUND:
                first_ring(b, o).start()

        @pl.when(core == 1)
        def _():
            first_far(b).start()

    def second(b):
        @pl.when(core == 0)
        def _():
            for o in AROUND:
                first_ring(b, o).wait()
            for slot, half in ((1, 1 - z_half), (0, z_half)):
                total = wide(chip_sums[b, half, y])
                for o in AROUND:
                    total = total + wide(first_in[b, 2 * (o - 1) + half])
                middle[b, slot] = total.astype(jnp.bfloat16)
                if slot == 1:
                    second_far(b).start()

        @pl.when(core == 1)
        def _():
            first_far(b).wait()
            for o in (1, 3, 2, 0):
                strip = lax.rem(y + o, 4)
                total = wide(chip_sums[b, z_half, strip]) + wide(first_in[b, strip])
                middle[b, o] = total.astype(jnp.bfloat16)
                if o:
                    second_ring(b, o).start()

    def finish(b):
        @pl.when(core == 0)
        def _():
            second_far(b).wait()
            own_sum[b] = wide(middle[b, 0]) + wide(second_in[b, 0])

        @pl.when(core == 1)
        def _():
            for o in AROUND:
                second_ring(b, o).wait()
            total = wide(middle[b, 0])
            for o in AROUND:
                total = total + wide(second_in[b, o - 1])
            own_sum[b] = total

        for d in range(KEPT):
            cols = pl.ds(pl.multiple_of(strip_of(d) * QT, QT), QT)
            sums[b, :, cols] = own_sum[b, :, d * QT : (d + 1) * QT]

    def mirror(group, d, other):
        to_core = lax.rem(core + other, 2)
        return pltpu.make_async_remote_copy(
            mirror_out.at[group, d - 1, to_core],
            mirror_in.at[group, d - 1, pl.ds(pl.multiple_of(core * 64, 64), 64), :],
            mir_send.at[group, d - 1, other], mir_recv.at[group, d - 1, other],
            device_id={"dp": strip_of(d), "outer": to_core}, device_id_type=MESH,
        )

    def send_mirror(group):
        low = lax.broadcasted_iota(jnp.int32, (64, QT), 1) < 64
        for d in (1, 2, 3):
            cols = slice(d * QT, (d + 1) * QT)
            if group == 0:
                one, two = own_sum[0, :, cols], own_sum[1, :, cols]
                pair = (
                    jnp.where(low, one, pltpu.roll(two, 64, 1)),
                    jnp.where(low, pltpu.roll(one, 64, 1), two),
                )
            else:
                pair = (own_sum[2, :, cols],) * 2
            for half in range(2):
                mirror_out[group, d - 1, half] = pair[half].astype(jnp.bfloat16)
        for d in (1, 2, 3):
            for other in range(2):
                mirror(group, d, other).start()

    def take_mirror(group):
        for d in (1, 2, 3):
            for other in range(2):
                mirror(group, d, other).wait()
        for d in (1, 2, 3):
            cols = pl.ds(pl.multiple_of(strip_of(STRIPS - d) * QT, QT), QT)
            flipped = wide(mirror_in[group, d - 1]).T
            if group == 0:
                sums[0, :, cols] = flipped[:64]
                sums[1, :, cols] = flipped[64:]
            else:
                turned[...] = flipped
                sums[2, :, cols] = turned[pl.ds(pl.multiple_of(core * 64, 64), 64), :]

    def first(k, carry):
        load(0, k).wait()
        dequantize(0, k)
        return carry

    lax.fori_loop(0, chunks, first, 0)
    for k in range(chunks):
        load(2, k).start()

    for b in range(NB):

        def step(j, carry):
            if b > 0:

                @pl.when(j == 1)
                def _():
                    chip_sum(b - 1)
                    if b == 1:
                        g_far.wait()
                        for o in AROUND:
                            g_next[o - 1].start()
                    else:
                        second(b - 2)

            if b == 0:

                @pl.when(j == 2)
                def _():
                    a_far.wait()
                    for o in (0, 2, 1):
                        a_next[o].start()

            if b + 1 < NB:
                load(b + 1, j).wait()
            gram(b, j)
            if b + 1 < NB:
                dequantize(b + 1, j)
            return carry

        lax.fori_loop(0, 4, step, 0)
        swap(b).start()
    chip_sum(NB - 1)
    second(NB - 2)
    finish(0)

    a_pair.append(a_copy(z_far(dp), core, 8, {"outer": 1 - core}))
    a_pair[-1].start()
    for o in (1, 2, 3):
        a_near[o - 1].wait()
        a_pair.append(a_copy(y_peer(4 - o), core, 8 + o, {"outer": 1 - core}))
        a_pair[-1].start()
    for o in (1, 2, 3):
        a_next[o - 1].wait()
        a_pair.append(a_copy(z_far(y_peer(4 - o)), core, 11 + o, {"outer": 1 - core}))
        a_pair[-1].start()
    for o in (1, 2, 3):
        g_near[o - 1].wait()
        g_next[o - 1].wait()
    for copy in a_pair:
        copy.wait()
    own_w.wait()

    def precondition(n):
        cols = pl.ds(n * 512, 512)
        right[...] = jnp.dot(
            weight[...], g_full[:, cols], preferred_element_type=jnp.float32
        ).astype(jnp.bfloat16)
        pre_out[:, cols] = jnp.dot(
            a_full[...], right[...], preferred_element_type=jnp.float32
        ).astype(jnp.bfloat16)

    precondition(0)
    second(NB - 1)
    finish(1)
    send_mirror(0)
    precondition(1)
    finish(2)
    send_mirror(1)
    take_mirror(0)
    take_mirror(1)
    a_out[0] = sums[0]
    g_out[0] = sums[1]
    g_out[1] = sums[2]


def blend(token_total, a_sum, g_sum, pre, prior, factor, a_stat, g_stat, new_a, new_g, pre_out, sem):
    copy = pltpu.make_async_copy(pre, pre_out, sem)
    copy.start()
    for total, old, stat, new in ((a_sum, prior, a_stat, new_a), (g_sum, factor, g_stat, new_g)):
        mean = total[...] / token_total
        stat[...] = mean
        new[...] = EMA_DECAY * old[...] + (1.0 - EMA_DECAY) * mean
    copy.wait()


def body(
    activations,
    act_scale,
    out_grads,
    gradient_tile_scale,
    prior_input_factor,
    g_factor,
    weight_grad,
    a_inverse,
    g_inverse,
):
    tokens = activations.shape[0]
    token_total = tokens * lax.axis_size("dp") * lax.axis_size("outer")
    vmem = pl.BlockSpec(memory_space=pltpu.VMEM)
    hbm = pl.BlockSpec(memory_space=pltpu.HBM)
    bf16, f32 = jnp.bfloat16, jnp.float32
    dma = pltpu.SemaphoreType.DMA
    a_sum, g_sum, preconditioned = pl.pallas_call(
        kernel,
        out_shape=(
            jax.ShapeDtypeStruct((1, 64, BLK), f32),
            jax.ShapeDtypeStruct((2, 64, BLK), f32),
            jax.ShapeDtypeStruct((BLK, BLK), bf16),
        ),
        in_specs=[hbm] * 7,
        out_specs=(vmem, vmem, vmem),
        scratch_shapes=[
            pltpu.SMEM(act_scale.shape[::-1], f32),
            pltpu.SMEM(gradient_tile_scale.shape, f32),
            pltpu.VMEM((2, tokens, BLK), bf16),
            pltpu.VMEM((tokens, BLK), bf16),
            pltpu.VMEM((tokens, BLK), bf16),
            pltpu.VMEM((12 * QT, tokens), bf16),
            pltpu.VMEM((12 * QT, tokens), bf16),
            pltpu.VMEM((2, NB, STRIPS, 64, WIDE), bf16),
            pltpu.VMEM((NB, STRIPS, 64, WIDE), bf16),
            pltpu.VMEM((NB, 2, 4, 64, WIDE), bf16),
            pltpu.VMEM((NB, 6, 64, WIDE), bf16),
            pltpu.VMEM((NB, 4, 64, WIDE), bf16),
            pltpu.VMEM((NB, 3, 64, WIDE), bf16),
            pltpu.VMEM((NB, 64, WIDE), f32),
            pltpu.VMEM((NB, 64, BLK), f32),
            pltpu.VMEM((2, 3, 2, 64, QT), bf16),
            pltpu.VMEM((2, 3, QT, QT), bf16),
            pltpu.VMEM((QT, QT), f32),
            pltpu.VMEM((BLK, BLK), bf16),
            pltpu.VMEM((BLK, BLK), bf16),
            pltpu.VMEM((BLK, BLK), bf16),
            pltpu.VMEM((BLK, 512), bf16),
            dma((NB, tokens // CHUNK)),
            dma((5,)),
            dma((7,)),
            dma((7,)),
            dma((15,)),
            dma((15,)),
            dma((NB,)),
            dma((NB,)),
            dma((NB, 4)),
            dma((NB, 4)),
            dma((NB, 4)),
            dma((NB, 4)),
            dma((2, 3, 2)),
            dma((2, 3, 2)),
        ],
        compiler_params=pltpu.CompilerParams(
            collective_id=0, has_side_effects=True, vmem_limit_bytes=50 << 20
        ),
        cost_estimate=pl.CostEstimate(
            flops=14_000_000_000, bytes_accessed=20_000_000, transcendentals=0
        ),
    )(
        *(
            pltpu.with_memory_space_constraint(value, pltpu.HBM)
            for value in (
                act_scale.T,
                gradient_tile_scale,
                activations,
                out_grads,
                weight_grad,
                a_inverse,
                g_inverse,
            )
        )
    )
    return pl.pallas_call(
        functools.partial(blend, token_total),
        out_shape=(
            jax.ShapeDtypeStruct((1, 64, BLK), f32),
            jax.ShapeDtypeStruct((2, 64, BLK), f32),
            jax.ShapeDtypeStruct((1, 64, BLK), f32),
            jax.ShapeDtypeStruct((2, 64, BLK), f32),
            jax.ShapeDtypeStruct((BLK, BLK), bf16),
        ),
        in_specs=[vmem] * 5,
        out_specs=(vmem, vmem, vmem, vmem, hbm),
        scratch_shapes=[dma],
        compiler_params=pltpu.CompilerParams(vmem_limit_bytes=8 << 20),
    )(a_sum, g_sum, preconditioned, prior_input_factor, g_factor)


def solution(mesh):
    return jax.shard_map(
        body,
        mesh=mesh,
        in_specs=(
            P(("dp", "outer"), "mp"),
            P(("dp", "outer"), "mp"),
            P(("dp", "outer"), "mp"),
            P(("dp", "outer"), "mp"),
            P("mp", ("dp", "outer"), None),
            P("mp", ("dp", "outer"), None),
            P("mp", ("dp", "outer")),
            P("mp", ("dp", "outer"), None),
            P(("dp", "outer"), "mp", None),
        ),
        out_specs=(
            P("mp", ("dp", "outer"), None),
            P("mp", ("dp", "outer"), None),
            P("mp", ("dp", "outer"), None),
            P("mp", ("dp", "outer"), None),
            P("mp", ("dp", "outer")),
        ),
        check_vma=False,
    )
```

time: 67.6 us -> 52.8 us (0.78)
  Pallas kernels: 59.9 us -> 52.1 us
  other arithmetic: 4.14 us -> 0 us
  local copies, waits for them, and re-layouts: 2.69 us -> 0.01 us
    pallas_call x1, Pallas kernels: 59.9 us -> 49.6 us  [body(): pl.pallas_call(kernel, out_shape=(jax.ShapeDtypeStruct((1, 64, BLK), f32)...]
    add x2 -> x0, other arithmetic: 4.14 us -> none  [the longest x1 2.19 us: body(): new_g_factor = EMA_DECAY * g_factor + (1.0 - EMA_DECAY) * g_stat]
    unnamed x8 -> x4, local copies, waits for them, and re-layouts: 2.69 us -> 0.01 us
    pallas_call x0 -> x1, Pallas kernels: none -> 2.47 us  [body(): pl.pallas_call(functools.partial(blend, token_total), out_shape=(jax.Shap...]
where the time goes in v2:
time: 52.8 us; the launch traced here: 52.7 us
  Pallas kernels  52.1 us (99%)
  between operations  0.67 us (1%)
    pallas_call x1, Pallas kernels, body(): pl.pallas_call(kernel, out_shape=(jax.ShapeDtypeStruct((1, 64, BLK), f32)...  49.6 us
    pallas_call x1, Pallas kernels, body(): pl.pallas_call(functools.partial(blend, token_total), out_shape=(jax.Shap...  2.47 us

profile of v2, /device:TPU:1, one launch (start us, length us, event | category | flops | bytes accessed | tf_op | source)
XLA Modules:
  0.0 52.7 jit_solution(17602358033556373996)
XLA Ops:
  0.6 0.0 copy-start
  0.6 0.0 copy-start.1
  0.7 49.6 %shard_map.128 = (f32[1,64,1024]{2,1,0:T(8,128)S(1)}, f32[2,64,1024]{2,1,0:T(8,128)S(1)}, bf16[1024,1024]{1,0:T(8,128)(2,1)S(1)}) custom-call(f32[8,16]{1,0:T(8,128)} %bitcast.1, f32[16,16]{1,0:T(8,128)} %grad_scale_hbm.1, bf16[2048,1024]{1,0:T(8,128)(2,1)} %act_hbm.1, bf16[2048,2048]{1,0:T(8,128)(2,1)} %grads_hbm.1, bf16[1024,1024]{1,0:T(8,128)(2,1)} %weight_hbm.1, ...), custom_call_target="tpu_custom_call" | custom-call | flops 14000000000 | bytes 20000000 | tf_op jit(solution)/shard_map/pallas_call | solution.py:453
  50.2 0.0 copy-done
  50.3 0.0 copy-done.1
  50.3 2.5 %shard_map.129 = (f32[1,64,1024]{2,1,0:T(8,128)}, f32[2,64,1024]{2,1,0:T(8,128)}, f32[1,64,1024]{2,1,0:T(8,128)}, f32[2,64,1024]{2,1,0:T(8,128)}, bf16[1024,1024]{1,0:T(8,128)(2,1)}) custom-call(f32[1,64,1024]{2,1,0:T(8,128)S(1)} %get-tuple-element.8.a_sum, f32[2,64,1024]{2,1,0:T(8,128)S(1)} %get-tuple-element.9.g_sum, ...), custom_call_target="tpu_custom_call" | custom-call | tf_op jit(solution)/shard_map/pallas_call | solution.py:520
Async XLA Ops:
  0.6 49.6 %copy-start = (f32[2,64,1024]{2,1,0:T(8,128)S(1)}, f32[2,64,1024]{2,1,0:T(8,128)}, u32[]{:S(2)}) copy-start(f32[2,64,1024]{2,1,0:T(8,128)} %factor.1) | copy-start | bytes 1572868
  0.6 49.6 %copy-start.1 = (f32[1,64,1024]{2,1,0:T(8,128)S(1)}, f32[1,64,1024]{2,1,0:T(8,128)}, u32[]{:S(2)}) copy-start(f32[1,64,1024]{2,1,0:T(8,128)} %prior.1) | copy-start | bytes 786436

commit v3 on v2

--- a/solution.py
+++ b/solution.py
@@ -17,6 +17,8 @@
 KEPT = 5
 WIDE = KEPT * QT
 AROUND = (1, 3, 2)
+RING = slice(0, 2 * QT)
+FAR = slice(2 * QT, WIDE)
 CHUNK = 512
 
 
@@ -41,9 +43,12 @@
     parts,
     swapped,
     chip_sums,
-    first_in,
-    middle,
-    second_in,
+    ring_in,
+    far_in,
+    ring_middle,
+    far_middle,
+    ring_second_in,
+    far_second_in,
     own_sum,
     sums,
     mirror_out,
@@ -208,28 +213,28 @@
 
     def first_ring(b, o):
         return pltpu.make_async_remote_copy(
-            chip_sums.at[b, :, lax.rem(y + o, 4)], first_in.at[b, pl.ds(2 * (o - 1), 2)],
+            chip_sums.at[b, :, lax.rem(y + o, 4), :, RING], ring_in.at[b, o - 1],
             first_send.at[b, o - 1], first_recv.at[b, o - 1],
             device_id={"dp": y_peer(o)}, device_id_type=MESH,
         )
 
     def first_far(b):
         return pltpu.make_async_remote_copy(
-            chip_sums.at[b, 1 - z_half], first_in.at[b, pl.ds(0, 4)],
+            chip_sums.at[b, 1 - z_half, :, :, FAR], far_in.at[b],
             first_send.at[b, 3], first_recv.at[b, 3],
             device_id={"dp": z_far(dp)}, device_id_type=MESH,
         )
 
     def second_ring(b, o):
         return pltpu.make_async_remote_copy(
-            middle.at[b, o], second_in.at[b, o - 1],
+            far_middle.at[b, o], far_second_in.at[b, o - 1],
             second_send.at[b, o - 1], second_recv.at[b, o - 1],
             device_id={"dp": y_peer(o)}, device_id_type=MESH,
         )
 
     def second_far(b):
         return pltpu.make_async_remote_copy(
-            middle.at[b, 1], second_in.at[b, 0], second_send.at[b, 3], second_recv.at[b, 3],
+            ring_middle.at[b, 1], ring_second_in.at[b], second_send.at[b, 3], second_recv.at[b, 3],
             device_id={"dp": z_far(dp)}, device_id_type=MESH,
         )
 
@@ -246,53 +251,37 @@
 
         lax.fori_loop(0, STRIPS, one, 0)
 
-        @pl.when(core == 0)
-        def _():
+        first_far(b).start()
+        for o in AROUND:
+            first_ring(b, o).start()
+
+    def second(b):
+        for o in AROUND:
+            first_ring(b, o).wait()
+        for slot, half in ((1, 1 - z_half), (0, z_half)):
+            total = wide(chip_sums[b, half, y, :, RING])
             for o in AROUND:
-                first_ring(b, o).start()
-
-        @pl.when(core == 1)
-        def _():
-            first_far(b).start()
-
-    def second(b):
-        @pl.when(core == 0)
-        def _():
-            for o in AROUND:
-                first_ring(b, o).wait()
-            for slot, half in ((1, 1 - z_half), (0, z_half)):
-                total = wide(chip_sums[b, half, y])
-                for o in AROUND:
-                    total = total + wide(first_in[b, 2 * (o - 1) + half])
-                middle[b, slot] = total.astype(jnp.bfloat16)
-                if slot == 1:
-                    second_far(b).start()
-
-        @pl.when(core == 1)
-        def _():
-            first_far(b).wait()
-            for o in (1, 3, 2, 0):
-                strip = lax.rem(y + o, 4)
-                total = wide(chip_sums[b, z_half, strip]) + wide(first_in[b, strip])
-                middle[b, o] = total.astype(jnp.bfloat16)
-                if o:
-                    second_ring(b, o).start()
+                total = total + wide(ring_in[b, o - 1, half])
+            ring_middle[b, slot] = total.astype(jnp.bfloat16)
+            if slot == 1:
+                second_far(b).start()
+        first_far(b).wait()
+        for o in (1, 3, 2, 0):
+            strip = lax.rem(y + o, 4)
+            total = wide(chip_sums[b, z_half, strip, :, FAR]) + wide(far_in[b, strip])
+            far_middle[b, o] = total.astype(jnp.bfloat16)
+            if o:
+                second_ring(b, o).start()
 
     def finish(b):
-        @pl.when(core == 0)
-        def _():
-            second_far(b).wait()
-            own_sum[b] = wide(middle[b, 0]) + wide(second_in[b, 0])
-
-        @pl.when(core == 1)
-        def _():
-            for o in AROUND:
-                second_ring(b, o).wait()
-            total = wide(middle[b, 0])
-            for o in AROUND:
-                total = total + wide(second_in[b, o - 1])
-            own_sum[b] = total
-
+        second_far(b).wait()
+        own_sum[b, :, RING] = wide(ring_middle[b, 0]) + wide(ring_second_in[b])
+        for o in AROUND:
+            second_ring(b, o).wait()
+        total = wide(far_middle[b, 0])
+        for o in AROUND:
+            total = total + wide(far_second_in[b, o - 1])
+        own_sum[b, :, FAR] = total
         for d in range(KEPT):
             cols = pl.ds(pl.multiple_of(strip_of(d) * QT, QT), QT)
             sums[b, :, cols] = own_sum[b, :, d * QT : (d + 1) * QT]
@@ -359,8 +348,6 @@
                         g_far.wait()
                         for o in AROUND:
                             g_next[o - 1].start()
-                    else:
-                        second(b - 2)
 
             if b == 0:
 
@@ -379,6 +366,7 @@
 
         lax.fori_loop(0, 4, step, 0)
         swap(b).start()
+    second(0)
     chip_sum(NB - 1)
     second(NB - 2)
     finish(0)
@@ -393,12 +381,6 @@
         a_next[o - 1].wait()
         a_pair.append(a_copy(z_far(y_peer(4 - o)), core, 11 + o, {"outer": 1 - core}))
         a_pair[-1].start()
-    for o in (1, 2, 3):
-        g_near[o - 1].wait()
-        g_next[o - 1].wait()
-    for copy in a_pair:
-        copy.wait()
-    own_w.wait()
 
     def precondition(n):
         cols = pl.ds(n * 512, 512)
@@ -409,13 +391,19 @@
             a_full[...], right[...], preferred_element_type=jnp.float32
         ).astype(jnp.bfloat16)
 
-    precondition(0)
     second(NB - 1)
     finish(1)
     send_mirror(0)
-    precondition(1)
+    own_w.wait()
+    for o in (1, 2, 3):
+        g_near[o - 1].wait()
+        g_next[o - 1].wait()
+    for copy in a_pair:
+        copy.wait()
+    precondition(0)
     finish(2)
     send_mirror(1)
+    precondition(1)
     take_mirror(0)
     take_mirror(1)
     a_out[0] = sums[0]
@@ -470,9 +458,12 @@
             pltpu.VMEM((2, NB, STRIPS, 64, WIDE), bf16),
             pltpu.VMEM((NB, STRIPS, 64, WIDE), bf16),
             pltpu.VMEM((NB, 2, 4, 64, WIDE), bf16),
-            pltpu.VMEM((NB, 6, 64, WIDE), bf16),
-            pltpu.VMEM((NB, 4, 64, WIDE), bf16),
-            pltpu.VMEM((NB, 3, 64, WIDE), bf16),
+            pltpu.VMEM((NB, 3, 2, 64, 2 * QT), bf16),
+            pltpu.VMEM((NB, 4, 64, WIDE - 2 * QT), bf16),
+            pltpu.VMEM((NB, 2, 64, 2 * QT), bf16),
+            pltpu.VMEM((NB, 4, 64, WIDE - 2 * QT), bf16),
+            pltpu.VMEM((NB, 64, 2 * QT), bf16),
+            pltpu.VMEM((NB, 3, 64, WIDE - 2 * QT), bf16),
             pltpu.VMEM((NB, 64, WIDE), f32),
             pltpu.VMEM((NB, 64, BLK), f32),
             pltpu.VMEM((2, 3, 2, 64, QT), bf16),

time: 52.8 us -> 51.1 us (0.968)
  Pallas kernels: 52.1 us -> 50.3 us
    pallas_call x1, Pallas kernels: 49.6 us -> 47.9 us  [body(): pl.pallas_call(kernel, out_shape=(jax.ShapeDtypeStruct((1, 64, BLK), f32)...]
where the time goes in v3:
time: 51.1 us; the launch traced here: 51 us
  Pallas kernels  50.3 us (98%)
  between operations  0.67 us (1%)
    pallas_call x1, Pallas kernels, body(): pl.pallas_call(kernel, out_shape=(jax.ShapeDtypeStruct((1, 64, BLK), f32)...  47.9 us
    pallas_call x1, Pallas kernels, body(): pl.pallas_call(functools.partial(blend, token_total), out_shape=(jax.Shap...  2.47 us

profile of v3, /device:TPU:1, one launch (start us, length us, event | category | flops | bytes accessed | tf_op | source)
XLA Modules:
  0.0 51.0 jit_solution(12970868182254175095)
XLA Ops:
  0.6 0.0 copy-start
  0.6 0.0 copy-start.1
  0.7 47.9 %shard_map.128 = (f32[1,64,1024]{2,1,0:T(8,128)S(1)}, f32[2,64,1024]{2,1,0:T(8,128)S(1)}, bf16[1024,1024]{1,0:T(8,128)(2,1)S(1)}) custom-call(f32[8,16]{1,0:T(8,128)} %bitcast.1, f32[16,16]{1,0:T(8,128)} %grad_scale_hbm.1, bf16[2048,1024]{1,0:T(8,128)(2,1)} %act_hbm.1, bf16[2048,2048]{1,0:T(8,128)(2,1)} %grads_hbm.1, bf16[1024,1024]{1,0:T(8,128)(2,1)} %weight_hbm.1, ...), custom_call_target="tpu_custom_call" | custom-call | flops 14000000000 | bytes 20000000 | tf_op jit(solution)/shard_map/pallas_call | solution.py:441
  48.5 0.0 copy-done
  48.5 0.0 copy-done.1
  48.6 2.5 %shard_map.129 = (f32[1,64,1024]{2,1,0:T(8,128)}, f32[2,64,1024]{2,1,0:T(8,128)}, f32[1,64,1024]{2,1,0:T(8,128)}, f32[2,64,1024]{2,1,0:T(8,128)}, bf16[1024,1024]{1,0:T(8,128)(2,1)}) custom-call(f32[1,64,1024]{2,1,0:T(8,128)S(1)} %get-tuple-element.8.a_sum, f32[2,64,1024]{2,1,0:T(8,128)S(1)} %get-tuple-element.9.g_sum, ...), custom_call_target="tpu_custom_call" | custom-call | tf_op jit(solution)/shard_map/pallas_call | solution.py:511
Async XLA Ops:
  0.6 47.9 %copy-start = (f32[2,64,1024]{2,1,0:T(8,128)S(1)}, f32[2,64,1024]{2,1,0:T(8,128)}, u32[]{:S(2)}) copy-start(f32[2,64,1024]{2,1,0:T(8,128)} %factor.1) | copy-start | bytes 1572868
  0.6 47.9 %copy-start.1 = (f32[1,64,1024]{2,1,0:T(8,128)S(1)}, f32[1,64,1024]{2,1,0:T(8,128)}, u32[]{:S(2)}) copy-start(f32[1,64,1024]{2,1,0:T(8,128)} %prior.1) | copy-start | bytes 786436
